TPU v7x, 32 devices: a whole 2x2x4 slice. The times are simulated.
32 devices in a mesh: dp: 8 (over z, y), mp: 4 (over x, core).
Axes of the slice: x: 2, y: 2, z: 4, core: 2. Of those that a mesh axis runs over, the one named last changes fastest.
Arguments:
- inputs: bfloat16 [8192, 768], P(('dp', 'mp')), may hold values from -6 to 6
- memory: bfloat16 [32768, 768], P(('dp', 'mp')), may hold values from -6 to 6
- target_len: int32 [64], P('dp'), may hold values from 8 to 114, as said below
- memory_len: int32 [64], P('dp'), may hold values from 32 to 512, as said below
- bucket_map: int32 [128], replicated, may hold values from 0 to 31, as said below
- self_gain: float32 [768], replicated, may hold values from 0.5 to 1.5
- self_query: bfloat16 [768, 768], P(None, 'mp'), may hold values from -0.02734375 to 0.02734375
- self_key: bfloat16 [768, 768], P(None, 'mp'), may hold values from -0.21875 to 0.21875
- self_value: bfloat16 [768, 768], P(None, 'mp'), may hold values from -0.21875 to 0.21875
- self_out: bfloat16 [768, 768], P('mp'), may hold values from -1.25 to 1.25
- bias_table: float32 [32, 12], P(None, 'mp'), may hold values from -4 to 4
- cross_gain: float32 [768], replicated, may hold values from 0.5 to 1.5
- cross_query: bfloat16 [768, 768], P(None, 'mp'), may hold values from -0.02734375 to 0.02734375
- cross_key: bfloat16 [768, 768], P(None, 'mp'), may hold values from -0.21875 to 0.21875
- cross_value: bfloat16 [768, 768], P(None, 'mp'), may hold values from -0.21875 to 0.21875
- cross_out: bfloat16 [768, 768], P('mp'), may hold values from -2.5 to 2.5
- feed_gain: float32 [768], replicated, may hold values from 0.5 to 1.5
- feed_input: bfloat16 [768, 3072], P(None, 'mp'), may hold values from -0.21875 to 0.21875
- feed_output: bfloat16 [3072, 768], P('mp'), may hold values from -0.15625 to 0.15625
- cotangent: bfloat16 [8192, 768], P(('dp', 'mp')), may hold values from -6 to 6
Outputs:
- layer_out: bfloat16 [8192, 768], P(('dp', 'mp'))
- inputs_grad: float32 [8192, 768], P(('dp', 'mp'))
- memory_grad: float32 [32768, 768], P(('dp', 'mp'))
- self_gain_grad: float32 [768], replicated
- self_query_grad: float32 [768, 768], P(None, 'mp')
- self_key_grad: float32 [768, 768], P(None, 'mp')
- self_value_grad: float32 [768, 768], P(None, 'mp')
- self_out_grad: float32 [768, 768], P('mp')
- bias_table_grad: float32 [32, 12], P(None, 'mp')
- cross_gain_grad: float32 [768], replicated
- cross_query_grad: float32 [768, 768], P(None, 'mp')
- cross_key_grad: float32 [768, 768], P(None, 'mp')
- cross_value_grad: float32 [768, 768], P(None, 'mp')
- cross_out_grad: float32 [768, 768], P('mp')
- feed_gain_grad: float32 [768], replicated
- feed_input_grad: float32 [768, 3072], P(None, 'mp')
- feed_output_grad: float32 [3072, 768], P('mp')
Inputs may be any that keep to these rules, and one draw needn't show every extreme that they name: bucket_map[d] is the bucket of a key d positions before its query: it equals d below 16, never falls as d grows, and reaches 31. An example's target rows at positions from target_len on are padding. An example's memory rows at positions from memory_len on are padding.
All inputs are finite; a program needn't handle non-finite values.
Results may differ from a plain program's by a relative error of at most 0.023.
Values may be sent and summed in bfloat16 or wider, within the bound.
No kernel may reach another device: no remote copies, remote signals or barrier semaphores. Data moves between devices by JAX's collectives and lax.ppermute only.
A program may use at most 128 MiB of HBM per device.

v0:
```python
import jax
import jax.numpy as jnp
from jax import lax
from jax.sharding import PartitionSpec as P

HEAD_DIM = 64
BUCKETS = 32
TGT_LEN = 128
MEM_LEN = 512
masked_fill = -1000000000.0
epsilon = 1e-06
highest = lax.Precision.HIGHEST
tanh_scale = 0.7978845608
cubic_term = 0.044715


def gelu_tanh(value):
    return 0.5 * value * (1.0 + jnp.tanh(tanh_scale * (value + cubic_term * value * value * value)))


def norm_forward(hidden, gain):
    scale = lax.rsqrt(jnp.mean(hidden * hidden, -1, keepdims=True) + epsilon)
    return (hidden * scale * gain, scale)


def norm_backward(hidden, scale, gain, upstream):
    weighted = gain * upstream
    return scale * weighted - hidden * scale**3 * jnp.mean(hidden * weighted, -1, keepdims=True)


def gather_normed(values):
    return lax.all_gather(values, "mp", axis=0, tiled=True)


def gather_upstream(values):
    return lax.all_gather(values, "mp", axis=0, tiled=True)


def project(rows, weight):
    return jnp.dot(rows, weight, preferred_element_type=jnp.float32).astype(jnp.bfloat16)


def back_project(grad_rows, weight):
    return lax.dot_general(
        grad_rows, weight, (((1,), (1,)), ((), ())), preferred_element_type=jnp.float32
    )


def weight_grad(rows, grad_rows):
    return jnp.einsum("rd,rc->dc", rows, grad_rows, preferred_element_type=jnp.float32)


def branch_sum(mixed, weight):
    return lax.psum_scatter(
        jnp.dot(mixed, weight, preferred_element_type=jnp.float32),
        "mp",
        scatter_dimension=0,
        tiled=True,
    )


def input_sum(weight_pairs, local_rows):
    summed = jnp.zeros((lax.axis_size("mp") * local_rows, weight_pairs[0][1].shape[0]), jnp.float32)
    for grad_rows, weight in weight_pairs:
        summed = summed + back_project(grad_rows, weight)
    return lax.psum_scatter(summed, "mp", scatter_dimension=0, tiled=True)


def split_heads(rows, groups, length):
    return rows.reshape(groups, length, rows.shape[1] // HEAD_DIM, HEAD_DIM)


def masked_scores(queries, key_blocks, extra, valid):
    scores = (
        jnp.einsum("eqhd,ekhd->ehqk", queries, key_blocks, preferred_element_type=jnp.float32)
        + extra
    )
    return jnp.where(valid, scores, masked_fill)


def attend(query_rows, key_rows, value_rows, extra, valid, key_len):
    groups = valid.shape[0]
    queries = split_heads(query_rows, groups, TGT_LEN)
    key_blocks = split_heads(key_rows, groups, key_len)
    value_blocks = split_heads(value_rows, groups, key_len)
    scores = masked_scores(queries, key_blocks, extra, valid)
    top_score = jnp.max(scores, -1, keepdims=True)
    log_total = top_score + jnp.log(jnp.sum(jnp.exp(scores - top_score), -1, keepdims=True))
    probs = jnp.exp(scores - log_total).astype(jnp.bfloat16)
    mixed = jnp.einsum("ehqk,ekhd->eqhd", probs, value_blocks, preferred_element_type=jnp.float32)
    return (mixed.astype(jnp.bfloat16).reshape(query_rows.shape), log_total)


def attend_back(query_rows, key_rows, value_rows, extra, valid, key_len, log_total, mixed_grad):
    groups = valid.shape[0]
    queries = split_heads(query_rows, groups, TGT_LEN)
    key_blocks = split_heads(key_rows, groups, key_len)
    value_blocks = split_heads(value_rows, groups, key_len)
    grad_blocks = split_heads(mixed_grad, groups, TGT_LEN)
    probs_full = jnp.exp(masked_scores(queries, key_blocks, extra, valid) - log_total)
    probs = probs_full.astype(jnp.bfloat16)
    value_grad = jnp.einsum(
        "ehqk,eqhd->ekhd", probs, grad_blocks, preferred_element_type=jnp.float32
    )
    prob_grad = jnp.einsum(
        "eqhd,ekhd->ehqk", grad_blocks, value_blocks, preferred_element_type=jnp.float32
    )
    score_grad = probs_full * (prob_grad - jnp.sum(probs_full * prob_grad, -1, keepdims=True))
    score_low = score_grad.astype(jnp.bfloat16)
    query_grad = jnp.einsum(
        "ehqk,ekhd->eqhd", score_low, key_blocks, preferred_element_type=jnp.float32
    )
    key_grad = jnp.einsum("ehqk,eqhd->ekhd", score_low, queries, preferred_element_type=jnp.float32)
    return (
        query_grad.astype(jnp.bfloat16).reshape(query_rows.shape),
        key_grad.astype(jnp.bfloat16).reshape(key_rows.shape),
        value_grad.astype(jnp.bfloat16).reshape(value_rows.shape),
        score_grad,
    )


def body(
    inputs,
    memory,
    target_len,
    memory_len,
    bucket_map,
    self_gain,
    self_query,
    self_key,
    self_value,
    self_out,
    bias_table,
    cross_gain,
    cross_query,
    cross_key,
    cross_value,
    cross_out,
    feed_gain,
    feed_input,
    feed_output,
    cotangent,
):
    local_rows = inputs.shape[0]
    positions = jnp.arange(TGT_LEN, dtype=jnp.int32)
    distance = jnp.maximum(positions[:, None] - positions[None, :], 0)
    lookup = distance[:, :, None] == positions[None, None, :]
    bucket_index = jnp.sum(jnp.where(lookup, bucket_map[None, None, :], 0), -1)
    causal = positions[None, :] <= positions[:, None]
    bucket_ids = jnp.arange(BUCKETS, dtype=jnp.int32)
    bucket_hot = (
        (bucket_index[:, :, None] == bucket_ids[None, None, :]) & causal[:, :, None]
    ).astype(jnp.float32)
    self_bias = jnp.einsum("qkb,bh->hqk", bucket_hot, bias_table, precision=highest)[None]
    self_valid = causal[None, None] & (
        positions[None, None, None, :] < target_len[:, None, None, None]
    )
    memory_pos = jnp.arange(MEM_LEN, dtype=jnp.int32)
    cross_valid = (memory_pos[None, :] < memory_len[:, None])[:, None, None, :]
    stream = inputs.astype(jnp.float32)
    normed_one, scale_one = norm_forward(stream, self_gain)
    gathered_one = gather_normed(normed_one.astype(jnp.bfloat16))
    self_queries = project(gathered_one, self_query)
    self_keys = project(gathered_one, self_key)
    self_values = project(gathered_one, self_value)
    self_mixed, self_total = attend(
        self_queries, self_keys, self_values, self_bias, self_valid, TGT_LEN
    )
    after_self = stream + branch_sum(self_mixed, self_out)
    normed_two, scale_two = norm_forward(after_self, cross_gain)
    gathered_two = gather_normed(normed_two.astype(jnp.bfloat16))
    memory_all = lax.all_gather(memory, "mp", axis=0, tiled=True)
    cross_queries = project(gathered_two, cross_query)
    cross_keys = project(memory_all, cross_key)
    cross_values = project(memory_all, cross_value)
    cross_mixed, cross_total = attend(
        cross_queries, cross_keys, cross_values, 0.0, cross_valid, MEM_LEN
    )
    after_cross = after_self + branch_sum(cross_mixed, cross_out)
    normed_three, scale_three = norm_forward(after_cross, feed_gain)
    gathered_three = gather_normed(normed_three.astype(jnp.bfloat16))
    pre_act = jnp.dot(gathered_three, feed_input, preferred_element_type=jnp.float32)
    act_value, act_pullback = jax.vjp(gelu_tanh, pre_act)
    activated = act_value.astype(jnp.bfloat16)
    result = after_cross + branch_sum(activated, feed_output)
    layer_out = result.astype(jnp.bfloat16)
    upstream = cotangent.astype(jnp.float32)
    feed_up = gather_upstream(cotangent)
    feed_output_part = weight_grad(activated, feed_up)
    hidden_grad = back_project(feed_up, feed_output)
    pre_grad = act_pullback(hidden_grad)[0].astype(jnp.bfloat16)
    feed_input_part = weight_grad(gathered_three, pre_grad)
    normed_three_grad = input_sum(((pre_grad, feed_input),), local_rows)
    feed_gain_part = jnp.sum(normed_three_grad * after_cross * scale_three, 0)
    grad_two = upstream + norm_backward(after_cross, scale_three, feed_gain, normed_three_grad)
    cross_up = gather_upstream(grad_two.astype(jnp.bfloat16))
    cross_out_part = weight_grad(cross_mixed, cross_up)
    mixed_two = back_project(cross_up, cross_out).astype(jnp.bfloat16)
    cross_q_grad, cross_k_grad, cross_v_grad, cross_score_grad = attend_back(
        cross_queries, cross_keys, cross_values, 0.0, cross_valid, MEM_LEN, cross_total, mixed_two
    )
    cross_query_part = weight_grad(gathered_two, cross_q_grad)
    cross_key_part = weight_grad(memory_all, cross_k_grad)
    cross_value_part = weight_grad(memory_all, cross_v_grad)
    late_totals = (
        cross_query_part,
        cross_key_part,
        cross_value_part,
        cross_out_part,
        feed_input_part,
        feed_output_part,
    )
    (
        cross_query_sum,
        cross_key_sum,
        cross_value_sum,
        cross_out_sum,
        feed_input_sum,
        feed_output_sum,
    ) = late_totals
    memory_grad = lax.psum_scatter(
        (back_project(cross_k_grad, cross_key) + back_project(cross_v_grad, cross_value)).astype(
            jnp.bfloat16
        ),
        "mp",
        scatter_dimension=0,
        tiled=True,
    ).astype(jnp.float32)
    normed_two_grad = input_sum(((cross_q_grad, cross_query),), local_rows)
    cross_gain_part = jnp.sum(normed_two_grad * after_self * scale_two, 0)
    grad_one = grad_two + norm_backward(after_self, scale_two, cross_gain, normed_two_grad)
    self_up = gather_upstream(grad_one.astype(jnp.bfloat16))
    self_out_part = weight_grad(self_mixed, self_up)
    mixed_one = back_project(self_up, self_out).astype(jnp.bfloat16)
    self_q_grad, self_k_grad, self_v_grad, self_score_grad = attend_back(
        self_queries, self_keys, self_values, self_bias, self_valid, TGT_LEN, self_total, mixed_one
    )
    bias_part = jnp.einsum("ehqk,qkb->bh", self_score_grad, bucket_hot, precision=highest)
    self_query_part = weight_grad(gathered_one, self_q_grad)
    self_key_part = weight_grad(gathered_one, self_k_grad)
    self_value_part = weight_grad(gathered_one, self_v_grad)
    normed_one_grad = input_sum(
        ((self_q_grad, self_query), (self_k_grad, self_key), (self_v_grad, self_value)), local_rows
    )
    self_gain_part = jnp.sum(normed_one_grad * stream * scale_one, 0)
    inputs_grad = grad_one + norm_backward(stream, scale_one, self_gain, normed_one_grad)
    gain_one, gain_two, gain_three = lax.psum(
        (self_gain_part, cross_gain_part, feed_gain_part), "mp"
    )
    every_total = lax.psum(
        (
            gain_one,
            self_query_part,
            self_key_part,
            self_value_part,
            self_out_part,
            bias_part,
            gain_two,
            cross_query_sum,
            cross_key_sum,
            cross_value_sum,
            cross_out_sum,
            gain_three,
            feed_input_sum,
            feed_output_sum,
        ),
        "dp",
    )
    (
        self_gain_sum,
        self_query_sum,
        self_key_sum,
        self_value_sum,
        self_out_sum,
        bias_sum,
        cross_gain_sum,
        cross_query_sum,
        cross_key_sum,
        cross_value_sum,
        cross_out_sum,
        feed_gain_sum,
        feed_input_sum,
        feed_output_sum,
    ) = every_total
    return (
        layer_out,
        inputs_grad,
        memory_grad,
        self_gain_sum,
        self_query_sum,
        self_key_sum,
        self_value_sum,
        self_out_sum,
        bias_sum,
        cross_gain_sum,
        cross_query_sum,
        cross_key_sum,
        cross_value_sum,
        cross_out_sum,
        feed_gain_sum,
        feed_input_sum,
        feed_output_sum,
    )


def solution(mesh):
    in_specs = (
        P(("dp", "mp"), None),
        P(("dp", "mp"), None),
        P("dp"),
        P("dp"),
        P(),
        P(),
        P(None, "mp"),
        P(None, "mp"),
        P(None, "mp"),
        P("mp", None),
        P(None, "mp"),
        P(),
        P(None, "mp"),
        P(None, "mp"),
        P(None, "mp"),
        P("mp", None),
        P(),
        P(None, "mp"),
        P("mp", None),
        P(("dp", "mp"), None),
    )
    out_specs = (
        P(("dp", "mp"), None),
        P(("dp", "mp"), None),
        P(("dp", "mp"), None),
        P(),
        P(None, "mp"),
        P(None, "mp"),
        P(None, "mp"),
        P("mp", None),
        P(None, "mp"),
        P(),
        P(None, "mp"),
        P(None, "mp"),
        P(None, "mp"),
        P("mp", None),
        P(),
        P(None, "mp"),
        P("mp", None),
    )
    return jax.shard_map(body, mesh=mesh, in_specs=in_specs, out_specs=out_specs, check_vma=False)
```

profile of v0, /device:TPU:0, one launch (start us, length us, event | category | flops | bytes accessed | tf_op | source)
XLA Modules:
  0.0 868.2 jit_solution(15124593207510473389)
XLA Ops:
  11.1 5.8 select_reduce_fusion
  21.8 11.7 %all-gather.8.cloned.1.call-done = bf16[1024,768]{1,0:T(8,128)(2,1)} async-done(((bf16[256,768]{1,0:T(8,128)(2,1)}), bf16[1024,768]{1,0:T(8,128)(2,1)}) %all-gather.8.cloned.1.call-update) | async-done | bytes 1572880 | tf_op jit(solution)/shard_map/all_gather | solution.py:32
  43.0 37.3 %reduce-scatter.8.cloned.1.call-done = f32[256,768]{1,0:T(8,128)} async-done(((f32[1024,768]{1,0:T(8,128)}), f32[256,768]{1,0:T(8,128)}) %reduce-scatter.8.cloned.1.call-update) | async-done | bytes 786448 | tf_op jit(solution)/shard_map/reduce_scatter | solution.py:54
  86.0 42.4 %all-gather.10.cloned.1.call-done = bf16[4096,768]{1,0:T(8,128)(2,1)} async-done(((bf16[1024,768]{1,0:T(8,128)(2,1)}), bf16[4096,768]{1,0:T(8,128)(2,1)}) %all-gather.10.cloned.1.call-update) | async-done | bytes 6291472 | tf_op jit(solution)/shard_map/all_gather | solution.py:172
  128.4 5.1 convolution_convert_fusion
  139.4 10.8 %all-gather.12.cloned.1.call-done = bf16[1024,768]{1,0:T(8,128)(2,1)} async-done(((bf16[256,768]{1,0:T(8,128)(2,1)}), bf16[1024,768]{1,0:T(8,128)(2,1)}) %all-gather.12.cloned.1.call-update) | async-done | bytes 1572880 | tf_op jit(solution)/shard_map/all_gather | solution.py:32
  163.4 37.5 %reduce-scatter.10.cloned.1.call-done = f32[256,768]{1,0:T(8,128)} async-done(((f32[1024,768]{1,0:T(8,128)}), f32[256,768]{1,0:T(8,128)}) %reduce-scatter.10.cloned.1.call-update) | async-done | bytes 786448 | tf_op jit(solution)/shard_map/reduce_scatter | solution.py:54
  204.6 17.4 %all-gather.16.cloned.1.call-done = bf16[1024,768]{1,0:T(8,128)(2,1)} async-done(((bf16[256,768]{1,0:T(8,128)(2,1)}), bf16[1024,768]{1,0:T(8,128)(2,1)}) %all-gather.16.cloned.1.call-update) | async-done | bytes 1572880 | tf_op jit(solution)/shard_map/all_gather | solution.py:36
  222.0 4.8 fusion.114
  226.8 17.0 %all-gather.14.cloned.1.call-done = bf16[1024,768]{1,0:T(8,128)(2,1)} async-done(((bf16[256,768]{1,0:T(8,128)(2,1)}), bf16[1024,768]{1,0:T(8,128)(2,1)}) %all-gather.14.cloned.1.call-update) | async-done | bytes 1572880 | tf_op jit(solution)/shard_map/all_gather | solution.py:32
  243.8 6.9 fusion.4
  251.9 3.1 fusion.115
  256.2 5.5 fusion.110
  261.8 31.3 %reduce-scatter.14.cloned.1.call-done = f32[256,768]{1,0:T(8,128)} async-done(((f32[1024,768]{1,0:T(8,128)}), f32[256,768]{1,0:T(8,128)}) %reduce-scatter.14.cloned.1.call-update) | async-done | bytes 786448 | tf_op jit(solution)/shard_map/reduce_scatter | solution.py:66
  295.6 38.2 %reduce-scatter.12.cloned.1.call-done = f32[256,768]{1,0:T(8,128)} async-done(((f32[1024,768]{1,0:T(8,128)}), f32[256,768]{1,0:T(8,128)}) %reduce-scatter.12.cloned.1.call-update) | async-done | bytes 786448 | tf_op jit(solution)/shard_map/reduce_scatter | solution.py:54
  333.8 2.8 fusion.112
  336.7 19.8 %all-gather.18.cloned.1.call-done = bf16[1024,768]{1,0:T(8,128)(2,1)} async-done(((bf16[256,768]{1,0:T(8,128)(2,1)}), bf16[1024,768]{1,0:T(8,128)(2,1)}) %all-gather.18.cloned.1.call-update) | async-done | bytes 1572880 | tf_op jit(solution)/shard_map/all_gather | solution.py:36
  358.8 5.7 multiply_reduce_fusion
  370.5 38.1 %reduce-scatter.16.cloned.1.call-done = f32[256,768]{1,0:T(8,128)} async-done(((f32[1024,768]{1,0:T(8,128)}), f32[256,768]{1,0:T(8,128)}) %reduce-scatter.16.cloned.1.call-update) | async-done | bytes 786448 | tf_op jit(solution)/shard_map/reduce_scatter | solution.py:66
  410.5 2.6 fusion.111
  413.7 4.0 fusion.9
  425.0 4.6 add_convert_fusion
  429.7 3.3 all-gather.20.cloned.1.call-done
  442.5 2.7 add_add_fusion
  445.5 5.3 fusion.117
  450.8 5.3 fusion.109
  471.4 22.7 %reduce-scatter.20.cloned.1.call-done = bf16[1024,768]{1,0:T(8,128)(2,1)} async-done(((bf16[4096,768]{1,0:T(8,128)(2,1)}), bf16[1024,768]{1,0:T(8,128)(2,1)}) %reduce-scatter.20.cloned.1.call-update) | async-done | bytes 1572880 | tf_op jit(solution)/shard_map/reduce_scatter | solution.py:221
  494.1 3.3 convert_element_type.162
  497.4 37.1 %reduce-scatter.18.cloned.1.call-done = f32[256,768]{1,0:T(8,128)} async-done(((f32[1024,768]{1,0:T(8,128)}), f32[256,768]{1,0:T(8,128)}) %reduce-scatter.18.cloned.1.call-update) | async-done | bytes 786448 | tf_op jit(solution)/shard_map/reduce_scatter | solution.py:66
  535.9 10.1 %all-reduce.2 = (f32[768]{0:T(1024)S(1)}, f32[768]{0:T(1024)S(1)}, f32[768]{0:T(1024)S(1)}) all-reduce(f32[768]{0:T(1024)S(1)} %get-tuple-element.21, f32[768]{0:T(1024)S(1)} %copy-done.77, f32[768]{0:T(1024)S(1)} %copy-done.76), channel_id=1, replica_groups=mesh['dp'=8,'mp'=4] {'mp'}, use_global_device_ids=true, to_apply=%region_21.22 | all-reduce | flops 2304 | bytes 18432 | tf_op jit(solution)/shard_map/psum | solution.py:247
  546.0 39.8 %all-reduce = (f32[768]{0:T(1024)}, f32[32,3]{0,1:T(4,128)}, f32[768]{0:T(1024)}, f32[768]{0:T(1024)}) all-reduce(f32[768]{0:T(1024)S(1)} %get-tuple-element.37, f32[32,3]{0,1:T(4,128)S(1)} %convolution_bitcast_fusion.3, f32[768]{0:T(1024)S(1)} %get-tuple-element.38, ...), channel_id=1, replica_groups=mesh['dp'=8,'mp'=4] {'dp'}, use_global_device_ids=true, to_apply=%region_22.23 | all-reduce | flops 2400 | bytes 19200 | tf_op jit(solution)/shard_map/psum | solution.py:250
  588.1 260.6 %all-reduce.5.cloned.1.call-done = (f32[768,192]{0,1:T(8,128)}, f32[768,192]{0,1:T(8,128)}, f32[768,192]{0,1:T(8,128)}, f32[192,768]{1,0:T(8,128)}, f32[768,192]...) async-done(((f32[768,192]{0,1:T(8,128)}, f32[768,192]{0,1:T(8,128)}, ...) | async-done | bytes 9437200 | tf_op jit(solution)/shard_map/psum | solution.py:250
  (310 shorter events, 110.3 us)
Async XLA Ops:
  7.2 236.6 %copy-start = (bf16[768,768]{1,0:T(8,128)(2,1)S(1)}, bf16[768,768]{1,0:T(8,128)(2,1)}, u32[]{:S(2)}) copy-start(bf16[768,768]{1,0:T(8,128)(2,1)} %param.37) | copy-start | bytes 3538948
  7.2 26.3 %all-gather.8.cloned.1.call-start = ((), (), s32[]{:S(2)}) async-start(), calls=%async_computation.7 | async-start | bytes 1966080 | tf_op jit(solution)/shard_map/all_gather | solution.py:32
  8.5 25.0 %copy-start.48 = (bf16[768,192]{0,1:T(8,128)(2,1)S(1)}, bf16[768,192]{0,1:T(8,128)(2,1)}, u32[]{:S(2)}) copy-start(bf16[768,192]{0,1:T(8,128)(2,1)} %param.27) | copy-start | bytes 884740
  11.0 69.3 %reduce-scatter.8.cloned.1.call-start = ((), (), s32[]{:S(2)}) async-start(), calls=%async_computation.8 | async-start | bytes 3932160 | tf_op jit(solution)/shard_map/reduce_scatter | solution.py:54
  20.1 15.8 %copy-start.46 = (bf16[768,192]{0,1:T(8,128)(2,1)S(1)}, bf16[768,192]{0,1:T(8,128)(2,1)}, u32[]{:S(2)}) copy-start(bf16[768,192]{0,1:T(8,128)(2,1)} %param.26) | copy-start | bytes 884740
  42.3 86.2 %all-gather.10.cloned.1.call-start = ((), (), s32[]{:S(2)}) async-start(), calls=%async_computation.9 | async-start | bytes 7864320 | tf_op jit(solution)/shard_map/all_gather | solution.py:172
  43.0 107.2 %all-gather.12.cloned.1.call-start = ((), (), s32[]{:S(2)}) async-start(), calls=%async_computation.10 | async-start | bytes 1966080 | tf_op jit(solution)/shard_map/all_gather | solution.py:32
  84.5 116.4 %reduce-scatter.10.cloned.1.call-start = ((), (), s32[]{:S(2)}) async-start(), calls=%async_computation.11 | async-start | bytes 3932160 | tf_op jit(solution)/shard_map/reduce_scatter | solution.py:54
  162.8 59.2 %all-gather.16.cloned.1.call-start = ((), (), s32[]{:S(2)}) async-start(), calls=%async_computation.14 | async-start | bytes 1966080 | tf_op jit(solution)/shard_map/all_gather | solution.py:36
  163.4 80.5 %all-gather.14.cloned.1.call-start = ((), (), s32[]{:S(2)}) async-start(), calls=%async_computation.12 | async-start | bytes 1966080 | tf_op jit(solution)/shard_map/all_gather | solution.py:32
  204.3 88.8 %reduce-scatter.14.cloned.1.call-start = ((), (), s32[]{:S(2)}) async-start(), calls=%async_computation.15 | async-start | bytes 3932160 | tf_op jit(solution)/shard_map/reduce_scatter | solution.py:66
  255.0 78.8 %reduce-scatter.12.cloned.1.call-start = ((), (), s32[]{:S(2)}) async-start(), calls=%async_computation.13 | async-start | bytes 3932160 | tf_op jit(solution)/shard_map/reduce_scatter | solution.py:54
  261.7 31.4 %copy-start.11 = (f32[256,768]{1,0:T(8,128)S(1)}, f32[256,768]{1,0:T(8,128)}, u32[]{:S(2)}) copy-start(f32[256,768]{1,0:T(8,128)} %copy-done.10) | copy-start | bytes 2359300
  261.7 72.0 %copy-start.39 = (bf16[256,768]{1,0:T(8,128)(2,1)S(1)}, bf16[256,768]{1,0:T(8,128)(2,1)}, u32[]{:S(2)}) copy-start(bf16[256,768]{1,0:T(8,128)(2,1)} %param.39) | copy-start | bytes 1179652
  261.8 94.7 %all-gather.18.cloned.1.call-start = ((), (), s32[]{:S(2)}) async-start(), calls=%async_computation.16 | async-start | bytes 1966080 | tf_op jit(solution)/shard_map/all_gather | solution.py:36
  336.6 22.2 %copy-start.63 = (f32[8,3,128]{2,1,0:T(4,128)S(1)}, f32[8,3,128]{2,1,0:T(4,128)}, u32[]{:S(2)}) copy-start(f32[8,3,128]{2,1,0:T(4,128)} %copy-done.62) | copy-start | bytes 36868
  336.6 22.2 %copy-start.69 = (pred[8,512]{1,0:T(8,128)(4,1)S(1)}, pred[8,512]{1,0:T(8,128)(4,1)}, u32[]{:S(2)}) copy-start(pred[8,512]{1,0:T(8,128)(4,1)} %iota_compare_fusion.3) | copy-start | bytes 12292
  336.6 71.9 %reduce-scatter.16.cloned.1.call-start = ((), (), s32[]{:S(2)}) async-start(), calls=%async_computation.17 | async-start | bytes 3932160 | tf_op jit(solution)/shard_map/reduce_scatter | solution.py:66
  370.4 38.1 %copy-start.73 = (f32[768]{0:T(1024)S(1)}, f32[768]{0:T(1024)}, u32[]{:S(2)}) copy-start(f32[768]{0:T(1024)} %param.31) | copy-start | bytes 9220
  370.4 38.1 %copy-start.79 = (f32[256]{0:T(256)S(1)}, f32[256]{0:T(256)}, u32[]{:S(2)}) copy-start(f32[256]{0:T(256)} %copy-done.78) | copy-start | bytes 3076
  370.4 40.1 %copy-start.82 = (f32[256]{0:T(256)S(1)}, f32[256]{0:T(256)}, u32[]{:S(2)}) copy-start(f32[256]{0:T(256)} %get-tuple-element.53) | copy-start | bytes 3076
  370.5 62.5 %all-gather.20.cloned.1.call-start = ((), (), s32[]{:S(2)}) async-start(), calls=%async_computation.18 | async-start | bytes 1966080 | tf_op jit(solution)/shard_map/all_gather | solution.py:36
  413.2 80.9 %reduce-scatter.20.cloned.1.call-start = ((), (), s32[]{:S(2)}) async-start(), calls=%async_computation.20 | async-start | bytes 7864320 | tf_op jit(solution)/shard_map/reduce_scatter | solution.py:221
  429.6 104.8 %reduce-scatter.18.cloned.1.call-start = ((), (), s32[]{:S(2)}) async-start(), calls=%async_computation.19 | async-start | bytes 3932160 | tf_op jit(solution)/shard_map/reduce_scatter | solution.py:66
  445.3 403.4 %all-reduce.5.cloned.1.call-start = ((), (), s32[]{:S(2)}) async-start(), calls=%async_computation.21 | async-start | bytes 18874368 | tf_op jit(solution)/shard_map/psum | solution.py:250
  471.4 63.1 %copy-start.12 = (bf16[256,768]{1,0:T(8,128)(2,1)S(1)}, bf16[256,768]{1,0:T(8,128)(2,1)}, u32[]{:S(2)}) copy-start(bf16[256,768]{1,0:T(8,128)(2,1)} %param.20) | copy-start | bytes 1179652
  471.4 63.1 %copy-start.72 = (f32[768]{0:T(1024)S(1)}, f32[768]{0:T(1024)}, u32[]{:S(2)}) copy-start(f32[768]{0:T(1024)} %param.25) | copy-start | bytes 9220
  471.4 63.1 %copy-start.75 = (f32[256]{0:T(256)S(1)}, f32[256]{0:T(256)}, u32[]{:S(2)}) copy-start(f32[256]{0:T(256)} %copy-done.74) | copy-start | bytes 3076
  471.4 64.5 %copy-start.76 = (f32[768]{0:T(1024)S(1)}, f32[768]{0:T(1024)}, u32[]{:S(2)}) copy-start(f32[768]{0:T(1024)} %get-tuple-element.17) | copy-start | bytes 9220
  471.4 64.5 %copy-start.77 = (f32[768]{0:T(1024)S(1)}, f32[768]{0:T(1024)}, u32[]{:S(2)}) copy-start(f32[768]{0:T(1024)} %get-tuple-element.19) | copy-start | bytes 9220
  471.4 114.4 %copy-start.36 = (f32[256,768]{1,0:T(8,128)S(1)}, f32[256,768]{1,0:T(8,128)}, u32[]{:S(2)}) copy-start(f32[256,768]{1,0:T(8,128)} %get-tuple-element.41) | copy-start | bytes 2359300
  471.4 114.4 %copy-start.81 = (f32[256]{0:T(256)S(1)}, f32[256]{0:T(256)}, u32[]{:S(2)}) copy-start(f32[256]{0:T(256)} %get-tuple-element.51) | copy-start | bytes 3076
  (76 other events, 237.9 us)
Sparse Core Ops, SparseCore 0:
  11.2 22.3 all-gather.7
  42.4 37.9 reduce-scatter.7
  82.0 46.3 all-gather.9
  130.5 19.6 all-gather.11
  162.9 37.9 reduce-scatter.9
  202.3 19.6 all-gather.15
  224.1 19.6 all-gather.13
  255.1 37.9 reduce-scatter.13
  295.8 37.9 reduce-scatter.11
  336.8 19.6 all-gather.17
  370.6 37.9 reduce-scatter.15
  413.3 19.6 all-gather.19
  435.7 58.3 reduce-scatter.19
  496.5 37.9 reduce-scatter.17
  543.3 305.2 all-reduce.4
where the time goes:
time: 875 us; the launch traced here: 868 us
  waiting for transfers between devices  627 us (72%)
  matrix products  99.8 us (11%)
  blocking collectives  49.9 us (6%)
  other arithmetic  40.4 us (5%)
  local copies, waits for them, and re-layouts  34.8 us (4%)
  between operations  15.2 us (2%)
    psum x1, waiting for transfers between devices, body(): lax.psum((gain_one, self_query_part, self_key_part, self_value_part, self...  261 us
    reduce_scatter x3, waiting for transfers between devices, branch_sum(): lax.psum_scatter(jnp.dot(mixed, weight, preferred_element_type=jnp.float3...  113 us
    reduce_scatter x3, waiting for transfers between devices, input_sum(): return lax.psum_scatter(summed, 'mp', scatter_dimension=0, tiled=True)  106 us
    all_gather x1, waiting for transfers between devices, body(): memory_all = lax.all_gather(memory, 'mp', axis=0, tiled=True)  42.4 us
    all_gather x3, waiting for transfers between devices, gather_upstream(): return lax.all_gather(values, 'mp', axis=0, tiled=True)  40.5 us
    psum x1, blocking collectives, body(): lax.psum((gain_one, self_query_part, self_key_part, self_value_part, self...  39.8 us
    all_gather x3, waiting for transfers between devices, gather_normed(): return lax.all_gather(values, 'mp', axis=0, tiled=True)  39.6 us
    unnamed x206, local copies, waits for them, and re-layouts  28.8 us
  transfers between devices with their start and end apart: 15, of which 15 were waited for; matrix products, arithmetic and copies ran while one was open for 11% of the time, Pallas kernels for 0%

commit v1 on v0

--- a/solution.py
+++ b/solution.py
@@ -14,6 +14,28 @@
 cubic_term = 0.044715
 
 
+def joined_along(blocks, dim):
+    shape = list(blocks.shape[1:])
+    shape[dim] *= blocks.shape[0]
+    return jnp.moveaxis(blocks, 0, dim).reshape(shape)
+
+
+def collect(array, axis, dim):
+    size = lax.axis_size(axis)
+    pairs = [(i, (i + 1) % size) for i in range(size)]
+    back = [(b, a) for a, b in pairs]
+    lower, upper = ([], [])
+    for hop in range(size - 1):
+        if hop % 2 == 0:
+            lower.append(lax.ppermute(lower[-1] if lower else array, axis, pairs))
+        else:
+            upper.append(lax.ppermute(upper[-1] if upper else array, axis, back))
+    pieces = jnp.stack([*lower[::-1], array, *upper])
+    shift = lax.axis_index(axis) - len(lower)
+    pieces = pieces[(jnp.arange(size) - shift) % size]
+    return joined_along(pieces, dim)
+
+
 def gelu_tanh(value):
     return 0.5 * value * (1.0 + jnp.tanh(tanh_scale * (value + cubic_term * value * value * value)))
 
@@ -33,7 +55,7 @@
 
 
 def gather_upstream(values):
-    return lax.all_gather(values, "mp", axis=0, tiled=True)
+    return collect(values, "mp", 0)
 
 
 def project(rows, weight):

time: 875 us -> 845 us (0.966)
  waiting for transfers between devices: 627 us -> 583 us
  local copies, waits for them, and re-layouts: 34.8 us -> 45.8 us
    ppermute x0 -> x9, waiting for transfers between devices: none -> 54.2 us  [the longest x6 53.7 us: collect(): lower.append(lax.ppermute(lower[-1] if lower else array, axis, pairs))]
    all_gather x3 -> x0, waiting for transfers between devices: 40.5 us -> none  [gather_upstream(): return lax.all_gather(values, 'mp', axis=0, tiled=True)]
    reduce_scatter x1, waiting for transfers between devices: 22.7 us -> 0.02 us  [body(): lax.psum_scatter((back_project(cross_k_grad, cross_key) + back_project(cr...]
    reduce_scatter x3, waiting for transfers between devices: 106 us -> 86.9 us  [input_sum(): return lax.psum_scatter(summed, 'mp', scatter_dimension=0, tiled=True)]
    all_gather x3, waiting for transfers between devices: 39.6 us -> 23.2 us  [gather_normed(): return lax.all_gather(values, 'mp', axis=0, tiled=True)]
    gather x0 -> x3, local copies, waits for them, and re-layouts: none -> 10.5 us  [collect(): pieces = pieces[(jnp.arange(size) - shift) % size]]
    unnamed x206 -> x222, local copies, waits for them, and re-layouts: 28.8 us -> 29.4 us
  transfers between devices with their start and end apart: 15 -> 21, of which waited for: 15 -> 17; matrix products, arithmetic and copies ran while one was open for 11% -> 12% of each run, Pallas kernels for 0% -> 0%
where the time goes in v1:
time: 845 us; the launch traced here: 838 us
  waiting for transfers between devices  583 us (69%)
  matrix products  93 us (11%)
  blocking collectives  49.9 us (6%)
  local copies, waits for them, and re-layouts  45.8 us (5%)
  other arithmetic  43.9 us (5%)
  between operations  15.5 us (2%)
    psum x1, waiting for transfers between devices, body(): lax.psum((gain_one, self_query_part, self_key_part, self_value_part, self...  262 us
    reduce_scatter x3, waiting for transfers between devices, branch_sum(): lax.psum_scatter(jnp.dot(mixed, weight, preferred_element_type=jnp.float3...  114 us
    reduce_scatter x3, waiting for transfers between devices, input_sum(): return lax.psum_scatter(summed, 'mp', scatter_dimension=0, tiled=True)  86.9 us
    ppermute x6, waiting for transfers between devices, collect(): lower.append(lax.ppermute(lower[-1] if lower else array, axis, pairs))  53.7 us
    all_gather x1, waiting for transfers between devices, body(): memory_all = lax.all_gather(memory, 'mp', axis=0, tiled=True)  42.4 us
    psum x1, blocking collectives, body(): lax.psum((gain_one, self_query_part, self_key_part, self_value_part, self...  39.8 us
    unnamed x222, local copies, waits for them, and re-layouts  29.4 us
    dot_general x10, matrix products, back_project(): lax.dot_general(grad_rows, weight, (((1,), (1,)), ((), ())), preferred_el...  23.8 us
  transfers between devices with their start and end apart: 21, of which 17 were waited for; matrix products, arithmetic and copies ran while one was open for 12% of the time, Pallas kernels for 0%

profile of v1, /device:TPU:0, one launch (start us, length us, event | category | flops | bytes accessed | tf_op | source)
XLA Modules:
  0.0 837.6 jit_solution(15409539745249560672)
XLA Ops:
  11.1 5.1 select_reduce_fusion
  21.2 12.4 %all-gather.5.cloned.1.call-done = bf16[1024,768]{1,0:T(8,128)(2,1)} async-done(((bf16[256,768]{1,0:T(8,128)(2,1)}), bf16[1024,768]{1,0:T(8,128)(2,1)}) %all-gather.5.cloned.1.call-update) | async-done | bytes 1572880 | tf_op jit(solution)/shard_map/all_gather | solution.py:54
  43.7 37.3 %reduce-scatter.8.cloned.1.call-done = f32[256,768]{1,0:T(8,128)} async-done(((f32[1024,768]{1,0:T(8,128)}), f32[256,768]{1,0:T(8,128)}) %reduce-scatter.8.cloned.1.call-update) | async-done | bytes 786448 | tf_op jit(solution)/shard_map/reduce_scatter | solution.py:76
  86.7 42.4 %all-gather.7.cloned.1.call-done = bf16[4096,768]{1,0:T(8,128)(2,1)} async-done(((bf16[1024,768]{1,0:T(8,128)(2,1)}), bf16[4096,768]{1,0:T(8,128)(2,1)}) %all-gather.7.cloned.1.call-update) | async-done | bytes 6291472 | tf_op jit(solution)/shard_map/all_gather | solution.py:194
  129.1 5.1 convolution_convert_fusion
  140.0 10.8 %all-gather.9.cloned.1.call-done = bf16[1024,768]{1,0:T(8,128)(2,1)} async-done(((bf16[256,768]{1,0:T(8,128)(2,1)}), bf16[1024,768]{1,0:T(8,128)(2,1)}) %all-gather.9.cloned.1.call-update) | async-done | bytes 1572880 | tf_op jit(solution)/shard_map/all_gather | solution.py:54
  163.5 38.1 %reduce-scatter.10.cloned.1.call-done = f32[256,768]{1,0:T(8,128)} async-done(((f32[1024,768]{1,0:T(8,128)}), f32[256,768]{1,0:T(8,128)}) %reduce-scatter.10.cloned.1.call-update) | async-done | bytes 786448 | tf_op jit(solution)/shard_map/reduce_scatter | solution.py:76
  206.8 10.5 %collective-permute-done = bf16[256,768]{1,0:T(8,128)(2,1)} collective-permute-done((bf16[256,768]{1,0:T(8,128)(2,1)}, bf16[256,768]{1,0:T(8,128)(2,1)}, u32[]{:S(2)}, u32[]{:S(2)}) %collective-permute-start) | collective-permute-done | bytes 393248 | tf_op jit(solution)/shard_map/ppermute | solution.py:30
  218.8 10.6 %collective-permute-done.1 = bf16[256,768]{1,0:T(8,128)(2,1)} collective-permute-done((bf16[256,768]{1,0:T(8,128)(2,1)}, bf16[256,768]{1,0:T(8,128)(2,1)}, u32[]{:S(2)}, u32[]{:S(2)}) %collective-permute-start.1) | collective-permute-done | bytes 393248 | tf_op jit(solution)/shard_map/ppermute | solution.py:30
  232.1 3.3 gather_fusion
  238.4 4.0 fusion.4
  243.7 3.1 fusion.117
  248.1 5.5 fusion.112
  253.7 31.3 %reduce-scatter.14.cloned.1.call-done = f32[256,768]{1,0:T(8,128)} async-done(((f32[1024,768]{1,0:T(8,128)}), f32[256,768]{1,0:T(8,128)}) %reduce-scatter.14.cloned.1.call-update) | async-done | bytes 786448 | tf_op jit(solution)/shard_map/reduce_scatter | solution.py:88
  287.5 38.2 %reduce-scatter.12.cloned.1.call-done = f32[256,768]{1,0:T(8,128)} async-done(((f32[1024,768]{1,0:T(8,128)}), f32[256,768]{1,0:T(8,128)}) %reduce-scatter.12.cloned.1.call-update) | async-done | bytes 786448 | tf_op jit(solution)/shard_map/reduce_scatter | solution.py:76
  330.2 9.1 %collective-permute-done.3 = bf16[256,768]{1,0:T(8,128)(2,1)S(1)} collective-permute-done((bf16[256,768]{1,0:T(8,128)(2,1)S(1)}, bf16[256,768]{1,0:T(8,128)(2,1)S(1)}, u32[]{:S(2)}, u32[]{:S(2)}) %collective-permute-start.3) | collective-permute-done | bytes 393248 | tf_op jit(solution)/shard_map/ppermute | solution.py:30
  339.3 7.2 collective-permute-done.4
  347.8 3.4 gather_fusion.1
  353.5 5.8 multiply_reduce_fusion
  366.0 4.0 fusion.9
  377.2 4.6 add_convert_fusion
  381.8 21.3 %reduce-scatter.16.cloned.1.call-done = f32[256,768]{1,0:T(8,128)} async-done(((f32[1024,768]{1,0:T(8,128)}), f32[256,768]{1,0:T(8,128)}) %reduce-scatter.16.cloned.1.call-update) | async-done | bytes 786448 | tf_op jit(solution)/shard_map/reduce_scatter | solution.py:88
  408.7 9.1 %collective-permute-done.6 = bf16[256,768]{1,0:T(8,128)(2,1)S(1)} collective-permute-done((bf16[256,768]{1,0:T(8,128)(2,1)S(1)}, bf16[256,768]{1,0:T(8,128)(2,1)S(1)}, u32[]{:S(2)}, u32[]{:S(2)}) %collective-permute-start.6) | collective-permute-done | bytes 393248 | tf_op jit(solution)/shard_map/ppermute | solution.py:30
  417.9 7.2 collective-permute-done.7
  426.4 3.8 gather_fusion.2
  441.6 4.9 fusion.119
  446.5 5.4 fusion.111
  467.0 3.4 convert_element_type.162
  470.4 34.3 %reduce-scatter.18.cloned.1.call-done = f32[256,768]{1,0:T(8,128)} async-done(((f32[1024,768]{1,0:T(8,128)}), f32[256,768]{1,0:T(8,128)}) %reduce-scatter.18.cloned.1.call-update) | async-done | bytes 786448 | tf_op jit(solution)/shard_map/reduce_scatter | solution.py:88
  506.1 10.1 %all-reduce.2 = (f32[768]{0:T(1024)S(1)}, f32[768]{0:T(1024)S(1)}, f32[768]{0:T(1024)S(1)}) all-reduce(f32[768]{0:T(1024)S(1)} %get-tuple-element.21, f32[768]{0:T(1024)S(1)} %copy-done.84, f32[768]{0:T(1024)S(1)} %copy-done.83), channel_id=1, replica_groups=mesh['dp'=8,'mp'=4] {'mp'}, use_global_device_ids=true, to_apply=%region_21.22 | all-reduce | flops 2304 | bytes 18432 | tf_op jit(solution)/shard_map/psum | solution.py:269
  516.3 39.8 %all-reduce = (f32[768]{0:T(1024)}, f32[32,3]{0,1:T(4,128)}, f32[768]{0:T(1024)}, f32[768]{0:T(1024)}) all-reduce(f32[768]{0:T(1024)S(1)} %get-tuple-element.37, f32[32,3]{0,1:T(4,128)S(1)} %convolution_bitcast_fusion.3, f32[768]{0:T(1024)S(1)} %get-tuple-element.38, ...), channel_id=1, replica_groups=mesh['dp'=8,'mp'=4] {'dp'}, use_global_device_ids=true, to_apply=%region_22.23 | all-reduce | flops 2400 | bytes 19200 | tf_op jit(solution)/shard_map/psum | solution.py:272
  557.2 261.7 %all-reduce.5.cloned.1.call-done = (f32[768,192]{0,1:T(8,128)}, f32[768,192]{0,1:T(8,128)}, f32[768,192]{0,1:T(8,128)}, f32[192,768]{1,0:T(8,128)}, f32[768,192]...) async-done(((f32[768,192]{0,1:T(8,128)}, f32[768,192]{0,1:T(8,128)}, ...) | async-done | bytes 9437200 | tf_op jit(solution)/shard_map/psum | solution.py:272
  (343 shorter events, 129.4 us)
Async XLA Ops:
  7.2 228.2 %copy-start = (bf16[768,768]{1,0:T(8,128)(2,1)S(1)}, bf16[768,768]{1,0:T(8,128)(2,1)}, u32[]{:S(2)}) copy-start(bf16[768,768]{1,0:T(8,128)(2,1)} %param.37) | copy-start | bytes 3538948
  7.2 26.3 %all-gather.5.cloned.1.call-start = ((), (), s32[]{:S(2)}) async-start(), calls=%async_computation.7 | async-start | bytes 1966080 | tf_op jit(solution)/shard_map/all_gather | solution.py:54
  11.0 70.0 %reduce-scatter.8.cloned.1.call-start = ((), (), s32[]{:S(2)}) async-start(), calls=%async_computation.8 | async-start | bytes 3932160 | tf_op jit(solution)/shard_map/reduce_scatter | solution.py:76
  42.9 86.2 %all-gather.7.cloned.1.call-start = ((), (), s32[]{:S(2)}) async-start(), calls=%async_computation.9 | async-start | bytes 7864320 | tf_op jit(solution)/shard_map/all_gather | solution.py:194
  43.7 107.2 %all-gather.9.cloned.1.call-start = ((), (), s32[]{:S(2)}) async-start(), calls=%async_computation.10 | async-start | bytes 1966080 | tf_op jit(solution)/shard_map/all_gather | solution.py:54
  85.2 116.3 %reduce-scatter.10.cloned.1.call-start = ((), (), s32[]{:S(2)}) async-start(), calls=%async_computation.11 | async-start | bytes 3932160 | tf_op jit(solution)/shard_map/reduce_scatter | solution.py:76
  163.4 72.0 %all-gather.11.cloned.1.call-start = ((), (), s32[]{:S(2)}) async-start(), calls=%async_computation.12 | async-start | bytes 1966080 | tf_op jit(solution)/shard_map/all_gather | solution.py:54
  204.9 80.1 %reduce-scatter.14.cloned.1.call-start = ((), (), s32[]{:S(2)}) async-start(), calls=%async_computation.14 | async-start | bytes 3932160 | tf_op jit(solution)/shard_map/reduce_scatter | solution.py:88
  205.0 12.3 %collective-permute-start = (bf16[256,768]{1,0:T(8,128)(2,1)}, bf16[256,768]{1,0:T(8,128)(2,1)}, u32[]{:S(2)}, u32[]{:S(2)}) collective-permute-start(bf16[256,768]{1,0:T(8,128)(2,1)} %param.39), channel_id=1, source_target_pairs={{0,1},{1,2},{2,3},{3,0},{4,5},{5,6},{6,7},{7,4},{8,9},{9,10},{10,1... | collective-permute-start | bytes 1179656 | tf_op jit(solution)/shard_map/ppermute | solution.py:30
  205.1 13.7 %collective-permute-start.2 = (bf16[256,768]{1,0:T(8,128)(2,1)}, bf16[256,768]{1,0:T(8,128)(2,1)}, u32[]{:S(2)}, u32[]{:S(2)}) collective-permute-start(bf16[256,768]{1,0:T(8,128)(2,1)} %param.39), channel_id=1, source_target_pairs={{1,0},{2,1},{3,2},{0,3},{5,4},{6,5},{7,6},{4,7},{9,8},{10,9},{11,1... | collective-permute-start | bytes 1179656 | tf_op jit(solution)/shard_map/ppermute | solution.py:32
  217.3 12.1 %collective-permute-start.1 = (bf16[256,768]{1,0:T(8,128)(2,1)}, bf16[256,768]{1,0:T(8,128)(2,1)}, u32[]{:S(2)}, u32[]{:S(2)}) collective-permute-start(bf16[256,768]{1,0:T(8,128)(2,1)} %collective-permute-done), channel_id=1, source_target_pairs={{0,1},{1,2},{2,3},{3,0},{4,5},{5,6},{6,7},{7,4},{8,9},{9,10},{10,1... | collective-permute-start | bytes 1179656 | tf_op jit(solution)/shard_map/ppermute | solution.py:30
  246.8 78.8 %reduce-scatter.12.cloned.1.call-start = ((), (), s32[]{:S(2)}) async-start(), calls=%async_computation.13 | async-start | bytes 3932160 | tf_op jit(solution)/shard_map/reduce_scatter | solution.py:76
  253.6 31.4 %copy-start.13 = (f32[256,768]{1,0:T(8,128)S(1)}, f32[256,768]{1,0:T(8,128)}, u32[]{:S(2)}) copy-start(f32[256,768]{1,0:T(8,128)} %copy-done.12) | copy-start | bytes 2359300
  253.6 72.1 %copy-start.42 = (bf16[256,768]{1,0:T(8,128)(2,1)S(1)}, bf16[256,768]{1,0:T(8,128)(2,1)}, u32[]{:S(2)}) copy-start(bf16[256,768]{1,0:T(8,128)(2,1)} %param.39) | copy-start | bytes 1179652
  253.6 149.5 %reduce-scatter.16.cloned.1.call-start = ((), (), s32[]{:S(2)}) async-start(), calls=%async_computation.15 | async-start | bytes 3932160 | tf_op jit(solution)/shard_map/reduce_scatter | solution.py:88
  328.4 10.8 %collective-permute-start.3 = (bf16[256,768]{1,0:T(8,128)(2,1)S(1)}, bf16[256,768]{1,0:T(8,128)(2,1)S(1)}, u32[]{:S(2)}, u32[]{:S(2)}) collective-permute-start(bf16[256,768]{1,0:T(8,128)(2,1)S(1)} %get-tuple-element.42), channel_id=1, source_target_pairs={{0,1},{1,2},{2,3},{3,0},{4,5},{5,6},{6,7},{7,4},{8,9},{9,10},{10,1... | collective-permute-start | bytes 1179656 | tf_op jit(solution)/shard_map/ppermute | solution.py:30
  328.4 10.8 %collective-permute-start.5 = (bf16[256,768]{1,0:T(8,128)(2,1)S(1)}, bf16[256,768]{1,0:T(8,128)(2,1)S(1)}, u32[]{:S(2)}, u32[]{:S(2)}) collective-permute-start(bf16[256,768]{1,0:T(8,128)(2,1)S(1)} %get-tuple-element.42), channel_id=1, source_target_pairs={{1,0},{2,1},{3,2},{0,3},{5,4},{6,5},{7,6},{4,7},{9,8},{10,9},{11,1... | collective-permute-start | bytes 1179656 | tf_op jit(solution)/shard_map/ppermute | solution.py:32
  339.3 7.2 collective-permute-start.4
  365.3 101.7 %reduce-scatter.20.cloned.1.call-start = ((), (), s32[]{:S(2)}) async-start(), calls=%async_computation.17 | async-start | bytes 7864320 | tf_op jit(solution)/shard_map/reduce_scatter | solution.py:243
  381.8 122.9 %reduce-scatter.18.cloned.1.call-start = ((), (), s32[]{:S(2)}) async-start(), calls=%async_computation.16 | async-start | bytes 3932160 | tf_op jit(solution)/shard_map/reduce_scatter | solution.py:88
  407.0 10.9 %collective-permute-start.6 = (bf16[256,768]{1,0:T(8,128)(2,1)S(1)}, bf16[256,768]{1,0:T(8,128)(2,1)S(1)}, u32[]{:S(2)}, u32[]{:S(2)}) collective-permute-start(bf16[256,768]{1,0:T(8,128)(2,1)S(1)} %get-tuple-element.40), channel_id=1, source_target_pairs={{0,1},{1,2},{2,3},{3,0},{4,5},{5,6},{6,7},{7,4},{8,9},{9,10},{10,1... | collective-permute-start | bytes 1179656 | tf_op jit(solution)/shard_map/ppermute | solution.py:30
  407.0 10.9 %collective-permute-start.8 = (bf16[256,768]{1,0:T(8,128)(2,1)S(1)}, bf16[256,768]{1,0:T(8,128)(2,1)S(1)}, u32[]{:S(2)}, u32[]{:S(2)}) collective-permute-start(bf16[256,768]{1,0:T(8,128)(2,1)S(1)} %get-tuple-element.40), channel_id=1, source_target_pairs={{1,0},{2,1},{3,2},{0,3},{5,4},{6,5},{7,6},{4,7},{9,8},{10,9},{11,1... | collective-permute-start | bytes 1179656 | tf_op jit(solution)/shard_map/ppermute | solution.py:32
  417.9 7.2 collective-permute-start.7
  441.3 377.5 %all-reduce.5.cloned.1.call-start = ((), (), s32[]{:S(2)}) async-start(), calls=%async_computation.18 | async-start | bytes 18874368 | tf_op jit(solution)/shard_map/psum | solution.py:272
  466.9 37.8 %copy-start.14 = (bf16[256,768]{1,0:T(8,128)(2,1)S(1)}, bf16[256,768]{1,0:T(8,128)(2,1)}, u32[]{:S(2)}) copy-start(bf16[256,768]{1,0:T(8,128)(2,1)} %param.20) | copy-start | bytes 1179652
  466.9 37.8 %copy-start.79 = (f32[768]{0:T(1024)S(1)}, f32[768]{0:T(1024)}, u32[]{:S(2)}) copy-start(f32[768]{0:T(1024)} %param.25) | copy-start | bytes 9220
  466.9 37.8 %copy-start.82 = (f32[256]{0:T(256)S(1)}, f32[256]{0:T(256)}, u32[]{:S(2)}) copy-start(f32[256]{0:T(256)} %copy-done.81) | copy-start | bytes 3076
  466.9 39.3 %copy-start.83 = (f32[768]{0:T(1024)S(1)}, f32[768]{0:T(1024)}, u32[]{:S(2)}) copy-start(f32[768]{0:T(1024)} %get-tuple-element.17) | copy-start | bytes 9220
  466.9 39.2 %copy-start.84 = (f32[768]{0:T(1024)S(1)}, f32[768]{0:T(1024)}, u32[]{:S(2)}) copy-start(f32[768]{0:T(1024)} %get-tuple-element.19) | copy-start | bytes 9220
  466.9 89.1 %copy-start.88 = (f32[256]{0:T(256)S(1)}, f32[256]{0:T(256)}, u32[]{:S(2)}) copy-start(f32[256]{0:T(256)} %get-tuple-element.51) | copy-start | bytes 3076
  466.9 89.1 %copy-start.39 = (f32[256,768]{1,0:T(8,128)S(1)}, f32[256,768]{1,0:T(8,128)}, u32[]{:S(2)}) copy-start(f32[256,768]{1,0:T(8,128)} %get-tuple-element.41) | copy-start | bytes 2359300
  504.7 51.4 %copy-start.37 = (f32[256,768]{1,0:T(8,128)S(1)}, f32[256,768]{1,0:T(8,128)}, u32[]{:S(2)}) copy-start(f32[256,768]{1,0:T(8,128)} %reduce-scatter.18.cloned.1.call-done) | copy-start | bytes 2359300
  (90 other events, 324.3 us)
Sparse Core Ops, SparseCore 0:
  11.2 22.3 all-gather.4
  43.1 37.9 reduce-scatter.7
  82.7 46.3 all-gather.6
  131.2 19.6 all-gather.8
  163.5 37.9 reduce-scatter.9
  205.1 23.6 all-gather.10
  247.0 37.9 reduce-scatter.13
  287.7 37.9 reduce-scatter.11
  365.4 37.6 reduce-scatter.15
  405.7 58.3 reduce-scatter.19
  466.6 37.9 reduce-scatter.17
  513.5 305.2 all-reduce.4
